TPU v7x, 256 devices: a 2x2x32 block of a 4x8x32 slice. The times are simulated.
256 devices in a mesh: parts: 4 (over x, y), row: 64 (over z, core).
Axes of the slice: x: 2, y: 2, z: 32, core: 2. Of those that a mesh axis runs over, the one named last changes fastest.
The devices are a block of a 4x8x32 slice.
Arguments:
- embeddings: bfloat16 [131072, 512], P(('parts', 'row')), parts along dimension 0, may hold values from -6 to 6
- sizes: int32 [512], P('parts'), parts along dimension 0, may hold values from 1 to 2048, 32768 in all
- order: int32 [131072], P('parts'), parts along dimension 0, may hold values from 0 to 32767, each once
Outputs:
- similarity: float32 [131072], P(('parts', 'row')), parts along dimension 0
There are 4 independent parts, one for each index of `parts`. A program takes and returns all parts, laid end to end along the dimension named above; each array names one. Nothing has to cross between parts.
Inputs may be any that keep to these rules, and one draw needn't show every extreme that they name: `sizes`: each cluster has 1 to 2048 items; they sum to 32768. `order`: each of 0 to 32767 once.
All inputs are finite; a program needn't handle non-finite values.
Results may differ from a plain program's by a relative error of at most 0.0014.
Values may be sent and summed in bfloat16 or wider, within the bound.
No kernel may reach another device: no remote copies, remote signals or barrier semaphores. Data moves between devices by JAX's collectives and lax.ppermute only.
A program may use at most 64 MiB of HBM per device.

v0:
```python
import jax
import jax.numpy as jnp
from jax import lax
from jax.sharding import PartitionSpec as P

REACH = 4


def shifted(x, axis, by):
    devices = lax.axis_size(axis)
    pairs = [(i, i + by) for i in range(devices) if 0 <= i + by < devices]
    return lax.ppermute(x, axis, pairs)


def cluster_of(ends, first, count):
    index = first + jnp.arange(count, dtype=jnp.int32)
    return jnp.sum((index[:, None] >= ends[None, :]).astype(jnp.int32), axis=1)


def local(embeddings, sizes, order):
    rows = embeddings.shape[0]
    devices = lax.axis_size("row")
    me = lax.axis_index("row")
    values = embeddings.astype(jnp.float32)
    unit = (values * lax.rsqrt(jnp.sum(values * values, axis=1, keepdims=True) + 1e-06)).astype(
        jnp.bfloat16
    )
    ends = jnp.cumsum(sizes)
    own_start = me * rows
    own_cluster = cluster_of(ends, own_start, rows)
    own_order = lax.dynamic_slice_in_dim(order, own_start, rows, 0)
    empty = jnp.full((rows,), -1.0, jnp.float32)
    count = unit.shape[0]
    update_scores = jnp.dot(unit, unit.T, preferred_element_type=jnp.float32)
    update_other = cluster_of(ends, own_start, count)
    update_ranks = lax.dynamic_slice_in_dim(order, own_start, count, 0)
    keep = (
        (own_cluster[:, None] == update_other[None, :])
        & (update_ranks[None, :] < own_order[:, None])
        & True
    )
    best = jnp.maximum(empty, jnp.max(jnp.where(keep, update_scores, jnp.float32(-1.0)), axis=1))
    for offset in range(1, REACH + 1):
        piece = shifted(unit, "row", offset)
        source = me - offset
        valid = source >= 0
        start = jnp.clip(source, 0, devices - 1) * rows
        scores = jnp.dot(unit, piece.T, preferred_element_type=jnp.float32)
        other = cluster_of(ends, start, rows)
        ranks = lax.dynamic_slice_in_dim(order, start, rows, 0)
        same = (own_cluster[:, None] == other[None, :]) & valid
        mine_keep = same & (ranks[None, :] < own_order[:, None])
        their_keep = same & (own_order[:, None] < ranks[None, :])
        best = jnp.maximum(best, jnp.max(jnp.where(mine_keep, scores, jnp.float32(-1.0)), axis=1))
        partner = jnp.max(jnp.where(their_keep, scores, jnp.float32(-1.0)), axis=0)
        returned = shifted(partner, "row", -offset)
        arrived = me + offset < devices
        best = jnp.maximum(best, jnp.where(arrived, returned, jnp.float32(-1.0)))
    return best


def solution(mesh):
    return jax.shard_map(
        local,
        mesh=mesh,
        in_specs=(P(("parts", "row"), None), P("parts"), P("parts")),
        out_specs=P(("parts", "row")),
        check_vma=False,
    )
```

profile of v0, /device:TPU:1252, one launch (start us, length us, event | category | flops | bytes accessed | tf_op | source)
XLA Modules:
  0.0 82.7 jit_solution(11553010934935190141)
XLA Ops:
  0.0 0.0 copy-start
  0.0 1.3 %fusion.1 = f32[512]{0:T(512)S(1)} fusion(bf16[512,512]{1,0:T(8,128)(2,1)} %param.3), kind=kLoop, calls=%fused_computation.4 | loop fusion | flops 785920 | bytes 526336 | tf_op jit(solution)/shard_map/reduce_sum | solution.py:25
  1.3 0.0 copy-done
  1.3 0.2 fusion.2
  1.5 2.7 %collective-permute-start.4 = (bf16[512,512]{1,0:T(8,128)(2,1)S(1)}, bf16[512,512]{1,0:T(8,128)(2,1)S(1)}, u32[]{:S(2)}, u32[]{:S(2)}) collective-permute-start(bf16[512,512]{1,0:T(8,128)(2,1)S(1)} %fusion.2), channel_id=1, source_target_pairs={{0,3},{1,4},{2,5},{3,6},{4,7},{5,8},{6,9},{7,10},{8,11},{9,12},{10... | collective-permute-start | bytes 1572872 | tf_op jit(solution)/shard_map/ppermute | solution.py:12
  4.2 3.8 %collective-permute-start.6 = (bf16[512,512]{1,0:T(8,128)(2,1)S(1)}, bf16[512,512]{1,0:T(8,128)(2,1)S(1)}, u32[]{:S(2)}, u32[]{:S(2)}) collective-permute-start(bf16[512,512]{1,0:T(8,128)(2,1)S(1)} %fusion.2), channel_id=1, source_target_pairs={{0,4},{1,5},{2,6},{3,7},{4,8},{5,9},{6,10},{7,11},{8,12},{9,13},{1... | collective-permute-start | bytes 1572872 | tf_op jit(solution)/shard_map/ppermute | solution.py:12
  8.0 3.2 %collective-permute-start.2 = (bf16[512,512]{1,0:T(8,128)(2,1)S(1)}, bf16[512,512]{1,0:T(8,128)(2,1)S(1)}, u32[]{:S(2)}, u32[]{:S(2)}) collective-permute-start(bf16[512,512]{1,0:T(8,128)(2,1)S(1)} %fusion.2), channel_id=1, source_target_pairs={{0,2},{1,3},{2,4},{3,5},{4,6},{5,7},{6,8},{7,9},{8,10},{9,11},{10,... | collective-permute-start | bytes 1572872 | tf_op jit(solution)/shard_map/ppermute | solution.py:12
  11.2 2.6 %collective-permute-start = (bf16[512,512]{1,0:T(8,128)(2,1)S(1)}, bf16[512,512]{1,0:T(8,128)(2,1)S(1)}, u32[]{:S(2)}, u32[]{:S(2)}) collective-permute-start(bf16[512,512]{1,0:T(8,128)(2,1)S(1)} %fusion.2), channel_id=1, source_target_pairs={{0,1},{1,2},{2,3},{3,4},{4,5},{5,6},{6,7},{7,8},{8,9},{9,10},{10,1... | collective-permute-start | bytes 1572872 | tf_op jit(solution)/shard_map/ppermute | solution.py:12
  13.9 0.0 copy-start.1
  13.9 0.6 copy-done.1
  14.5 0.1 copy.22
  14.7 0.2 reduce-window.8
  14.8 0.1 reduce
  14.9 0.9 %fusion.3 = (s32[512]{0:T(512)S(1)}, s32[512]{0:T(512)S(1)}, s32[512]{0:T(512)S(1)}, s32[512]{0:T(512)S(1)}, s32[512]{0:T(512)S(1)}) fusion(s32[32768]{0:T(1024)} %param.5, s32[]{:T(128)S(6)} %select_n.87, s32[]{:T(128)S(6)} %select_n.77, s32[]{:T(128)S(6)} %select_n.72, s32[]{:T(128)S(6)} %select_n.70, s32[]{:T(128)S(6)} %select_n.82), kind=kLoop, calls=%fused_computation.30 | loop fusion | bytes 20500 | tf_op jit(solution)/shard_map/dynamic_slice | solution.py:50
  15.8 0.9 %convert_reduce_fusion.3 = (s32[512]{0:T(512)S(1)}, s32[512]{0:T(512)S(1)}, s32[512]{0:T(512)S(1)}, s32[512]{0:T(512)S(1)}, s32[512]{0:T(512)S(1)}) fusion(s32[128]{0:T(128)S(1)} %reduce, s32[512]{0:T(512)S(1)} %get-tuple-element.32, s32[512]{0:T(512)S(1)} %get-tuple-element.31, s32[512]{0:T(512)S(1)} %get-tuple-element.30, s32[512]{0:T(512)S(1)} %get-tuple-element.29, ...), kind=kLoop, calls=%fused_computation.21 | loop fusion | flops 980480 | bytes 20992 | tf_op jit(solution)/shard_map/reduce_sum | solution.py:17
  16.7 17.9 %collective-permute-done.4 = bf16[512,512]{1,0:T(8,128)(2,1)S(1)} collective-permute-done((bf16[512,512]{1,0:T(8,128)(2,1)S(1)}, bf16[512,512]{1,0:T(8,128)(2,1)S(1)}, u32[]{:S(2)}, u32[]{:S(2)}) %collective-permute-start.4) | collective-permute-done | bytes 524320 | tf_op jit(solution)/shard_map/ppermute | solution.py:12
  34.6 0.5 fusion.5
  35.1 10.4 %collective-permute-done.6 = bf16[512,512]{1,0:T(8,128)(2,1)S(1)} collective-permute-done((bf16[512,512]{1,0:T(8,128)(2,1)S(1)}, bf16[512,512]{1,0:T(8,128)(2,1)S(1)}, u32[]{:S(2)}, u32[]{:S(2)}) %collective-permute-start.6) | collective-permute-done | bytes 524320 | tf_op jit(solution)/shard_map/ppermute | solution.py:12
  45.4 0.5 fusion.6
  45.9 10.6 %collective-permute-done.2 = bf16[512,512]{1,0:T(8,128)(2,1)S(1)} collective-permute-done((bf16[512,512]{1,0:T(8,128)(2,1)S(1)}, bf16[512,512]{1,0:T(8,128)(2,1)S(1)}, u32[]{:S(2)}, u32[]{:S(2)}) %collective-permute-start.2) | collective-permute-done | bytes 524320 | tf_op jit(solution)/shard_map/ppermute | solution.py:12
  56.5 0.5 fusion.4
  57.0 5.7 %collective-permute-done = bf16[512,512]{1,0:T(8,128)(2,1)S(1)} collective-permute-done((bf16[512,512]{1,0:T(8,128)(2,1)S(1)}, bf16[512,512]{1,0:T(8,128)(2,1)S(1)}, u32[]{:S(2)}, u32[]{:S(2)}) %collective-permute-start) | collective-permute-done | bytes 524320 | tf_op jit(solution)/shard_map/ppermute | solution.py:12
  62.7 3.0 %select_reduce_fusion.7 = (f32[512]{0:T(512)S(1)}, f32[512]{0:T(512)S(1)}, f32[512]{0:T(512)S(1)}, f32[512]{0:T(512)S(1)}, f32[512]{0:T(512)S(1)}, /*index=5*/f32[512]{0:T(512)S(1)}, f32[512]{0:T(512)S(1)}, f32[512]{0:T(512)S(1)}) fusion(s32[512]{0:T(512)S(1)} %get-tuple-element.27, s32[512]{0:T(512)S(1)} %get-tuple-element.23, ...), kind=kOutput, calls=%fused_computation.13 | convolution fusion | flops 278917120 | bytes 4231172 | tf_op jit(solution)/shard_map/dot_general | solution.py:48
  65.7 2.0 %collective-permute-start.1 = (f32[512]{0:T(512)S(1)}, f32[512]{0:T(512)S(1)}, u32[]{:S(2)}, u32[]{:S(2)}) collective-permute-start(f32[512]{0:T(512)S(1)} %get-tuple-element.6), channel_id=1, source_target_pairs={{1,0},{2,1},{3,2},{4,3},{5,4},{6,5},{7,6},{8,7},{9,8},{10,9},{11,1... | collective-permute-start | bytes 6152 | tf_op jit(solution)/shard_map/ppermute | solution.py:12
  67.6 2.7 %collective-permute-start.3 = (f32[512]{0:T(512)S(1)}, f32[512]{0:T(512)S(1)}, u32[]{:S(2)}, u32[]{:S(2)}) collective-permute-start(f32[512]{0:T(512)S(1)} %get-tuple-element.13), channel_id=1, source_target_pairs={{2,0},{3,1},{4,2},{5,3},{6,4},{7,5},{8,6},{9,7},{10,8},{11,9},{12,... | collective-permute-start | bytes 6152 | tf_op jit(solution)/shard_map/ppermute | solution.py:12
  70.3 4.2 %collective-permute-start.5 = (f32[512]{0:T(512)S(1)}, f32[512]{0:T(512)S(1)}, u32[]{:S(2)}, u32[]{:S(2)}) collective-permute-start(f32[512]{0:T(512)S(1)} %get-tuple-element.15), channel_id=1, source_target_pairs={{3,0},{4,1},{5,2},{6,3},{7,4},{8,5},{9,6},{10,7},{11,8},{12,9},{13... | collective-permute-start | bytes 6152 | tf_op jit(solution)/shard_map/ppermute | solution.py:12
  74.5 2.1 %collective-permute-start.7 = (f32[512]{0:T(512)S(1)}, f32[512]{0:T(512)S(1)}, u32[]{:S(2)}, u32[]{:S(2)}) collective-permute-start(f32[512]{0:T(512)S(1)} %get-tuple-element.17), channel_id=1, source_target_pairs={{4,0},{5,1},{6,2},{7,3},{8,4},{9,5},{10,6},{11,7},{12,8},{13,9},{1... | collective-permute-start | bytes 6152 | tf_op jit(solution)/shard_map/ppermute | solution.py:12
  76.7 0.5 fusion
  77.2 0.0 collective-permute-done.1
  77.2 0.0 collective-permute-done.3
  77.2 0.0 collective-permute-done.5
  77.2 4.9 %collective-permute-done.7 = f32[512]{0:T(512)S(1)} collective-permute-done((f32[512]{0:T(512)S(1)}, f32[512]{0:T(512)S(1)}, u32[]{:S(2)}, u32[]{:S(2)}) %collective-permute-start.7) | collective-permute-done | bytes 2080 | tf_op jit(solution)/shard_map/ppermute | solution.py:12
  82.1 0.6 select_maximum_fusion
  (4 shorter events, 0.0 us)
Async XLA Ops:
  0.0 1.3 %copy-start = (bf16[512,512]{1,0:T(8,128)(2,1)S(1)}, bf16[512,512]{1,0:T(8,128)(2,1)}, u32[]{:S(2)}) copy-start(bf16[512,512]{1,0:T(8,128)(2,1)} %param.3) | copy-start | bytes 1572868
  1.5 33.1 %collective-permute-start.4 = (bf16[512,512]{1,0:T(8,128)(2,1)S(1)}, bf16[512,512]{1,0:T(8,128)(2,1)S(1)}, u32[]{:S(2)}, u32[]{:S(2)}) collective-permute-start(bf16[512,512]{1,0:T(8,128)(2,1)S(1)} %fusion.2), channel_id=1, source_target_pairs={{0,3},{1,4},{2,5},{3,6},{4,7},{5,8},{6,9},{7,10},{8,11},{9,12},{10... | collective-permute-start | bytes 1572872 | tf_op jit(solution)/shard_map/ppermute | solution.py:12
  4.2 41.2 %collective-permute-start.6 = (bf16[512,512]{1,0:T(8,128)(2,1)S(1)}, bf16[512,512]{1,0:T(8,128)(2,1)S(1)}, u32[]{:S(2)}, u32[]{:S(2)}) collective-permute-start(bf16[512,512]{1,0:T(8,128)(2,1)S(1)} %fusion.2), channel_id=1, source_target_pairs={{0,4},{1,5},{2,6},{3,7},{4,8},{5,9},{6,10},{7,11},{8,12},{9,13},{1... | collective-permute-start | bytes 1572872 | tf_op jit(solution)/shard_map/ppermute | solution.py:12
  8.0 48.5 %collective-permute-start.2 = (bf16[512,512]{1,0:T(8,128)(2,1)S(1)}, bf16[512,512]{1,0:T(8,128)(2,1)S(1)}, u32[]{:S(2)}, u32[]{:S(2)}) collective-permute-start(bf16[512,512]{1,0:T(8,128)(2,1)S(1)} %fusion.2), channel_id=1, source_target_pairs={{0,2},{1,3},{2,4},{3,5},{4,6},{5,7},{6,8},{7,9},{8,10},{9,11},{10,... | collective-permute-start | bytes 1572872 | tf_op jit(solution)/shard_map/ppermute | solution.py:12
  11.2 51.6 %collective-permute-start = (bf16[512,512]{1,0:T(8,128)(2,1)S(1)}, bf16[512,512]{1,0:T(8,128)(2,1)S(1)}, u32[]{:S(2)}, u32[]{:S(2)}) collective-permute-start(bf16[512,512]{1,0:T(8,128)(2,1)S(1)} %fusion.2), channel_id=1, source_target_pairs={{0,1},{1,2},{2,3},{3,4},{4,5},{5,6},{6,7},{7,8},{8,9},{9,10},{10,1... | collective-permute-start | bytes 1572872 | tf_op jit(solution)/shard_map/ppermute | solution.py:12
  13.9 0.7 copy-start.1
  65.7 11.5 %collective-permute-start.1 = (f32[512]{0:T(512)S(1)}, f32[512]{0:T(512)S(1)}, u32[]{:S(2)}, u32[]{:S(2)}) collective-permute-start(f32[512]{0:T(512)S(1)} %get-tuple-element.6), channel_id=1, source_target_pairs={{1,0},{2,1},{3,2},{4,3},{5,4},{6,5},{7,6},{8,7},{9,8},{10,9},{11,1... | collective-permute-start | bytes 6152 | tf_op jit(solution)/shard_map/ppermute | solution.py:12
  67.6 9.6 %collective-permute-start.3 = (f32[512]{0:T(512)S(1)}, f32[512]{0:T(512)S(1)}, u32[]{:S(2)}, u32[]{:S(2)}) collective-permute-start(f32[512]{0:T(512)S(1)} %get-tuple-element.13), channel_id=1, source_target_pairs={{2,0},{3,1},{4,2},{5,3},{6,4},{7,5},{8,6},{9,7},{10,8},{11,9},{12,... | collective-permute-start | bytes 6152 | tf_op jit(solution)/shard_map/ppermute | solution.py:12
  70.3 6.9 %collective-permute-start.5 = (f32[512]{0:T(512)S(1)}, f32[512]{0:T(512)S(1)}, u32[]{:S(2)}, u32[]{:S(2)}) collective-permute-start(f32[512]{0:T(512)S(1)} %get-tuple-element.15), channel_id=1, source_target_pairs={{3,0},{4,1},{5,2},{6,3},{7,4},{8,5},{9,6},{10,7},{11,8},{12,9},{13... | collective-permute-start | bytes 6152 | tf_op jit(solution)/shard_map/ppermute | solution.py:12
  74.5 7.6 %collective-permute-start.7 = (f32[512]{0:T(512)S(1)}, f32[512]{0:T(512)S(1)}, u32[]{:S(2)}, u32[]{:S(2)}) collective-permute-start(f32[512]{0:T(512)S(1)} %get-tuple-element.17), channel_id=1, source_target_pairs={{4,0},{5,1},{6,2},{7,3},{8,4},{9,5},{10,6},{11,7},{12,8},{13,9},{1... | collective-permute-start | bytes 6152 | tf_op jit(solution)/shard_map/ppermute | solution.py:12
where the time goes:
time: 83.1 us; the launch traced here: 82.7 us
  waiting for transfers between devices  49.5 us (60%)
  starting transfers between devices  23.2 us (28%)
  matrix products  4.88 us (6%)
  other arithmetic  3.25 us (4%)
  local copies, waits for them, and re-layouts  1.63 us (2%)
    ppermute x8, waiting for transfers between devices, shifted(): return lax.ppermute(x, axis, pairs)  49.5 us
    ppermute x8, starting transfers between devices, shifted(): return lax.ppermute(x, axis, pairs)  23.2 us
    dot_general x4, matrix products, local(): scores = jnp.dot(unit, piece.T, preferred_element_type=jnp.float32)  4.37 us
  transfers between devices with their start and end apart: 8, of which 5 were waited for; matrix products, arithmetic and copies ran while one was open for 5% of the time, Pallas kernels for 0%

commit v1 on v0

v1 whole, which is shorter than its diff:
```python
import functools

import jax
import jax.numpy as jnp
from jax import lax
from jax.experimental import pallas as pl
from jax.experimental.pallas import tpu as pltpu
from jax.sharding import PartitionSpec as P

STEP = 64
LANES = 128
VMEM = pl.BlockSpec(memory_space=pltpu.VMEM)


def shifted(x, by):
    devices = lax.axis_size("row")
    return lax.ppermute(x, "row", [(i, i + by) for i in range(devices) if 0 <= i + by < devices])


def normalise(src, dst, at):
    for s in range(0, src.shape[0], STEP):
        v = src[s : s + STEP, :].astype(jnp.float32)
        v = v * lax.rsqrt(jnp.sum(v * v, axis=1, keepdims=True) + 1e-06)
        dst[at + s : at + s + STEP, :] = v.astype(jnp.bfloat16)


def columns(key):
    return jnp.transpose(jnp.broadcast_to(key, (LANES, key.shape[1])))


def to_row(best):
    return jnp.max(jnp.transpose(best), axis=0, keepdims=True)


def score(x, y, out):
    out[...] = lax.dot_general(x, y, (((1,), (1,)), ((), ())), preferred_element_type=jnp.float32)


def pair_max(s, c1, c2, k1, k2, rowbest):
    n = k1.shape[1]
    over = [jnp.full((8, LANES), -1.0, jnp.float32) for _ in range(n // LANES)]
    for a in range(0, s.shape[0], STEP):
        x1, x2 = c1[a : a + STEP, :], c2[a : a + STEP, :]
        mine = rowbest[a : a + STEP, :]
        for t in range(n // LANES):
            v = s[a : a + STEP, t * LANES : (t + 1) * LANES]
            y1, y2 = k1[:, t * LANES : (t + 1) * LANES], k2[:, t * LANES : (t + 1) * LANES]
            theirs = jnp.where(x1 < y1, v, -1.0)
            over[t] = jnp.maximum(over[t], jnp.max(theirs.reshape(STEP // 8, 8, LANES), axis=0))
            mine = jnp.maximum(mine, jnp.where(y2 < x2, v, -1.0))
        rowbest[a : a + STEP, :] = mine
    return jnp.concatenate([jnp.max(o, axis=0, keepdims=True) for o in over], axis=1)


def own_kernel(own, keys, unit, best, s, c1, c2):
    normalise(own, unit, 0)
    k1, k2 = keys[2:3, :], keys[10:11, :]
    c1[...] = columns(k1)
    c2[...] = columns(k2)
    score(unit[...], unit[...], s)
    n = k1.shape[1]
    over = [jnp.full((8, LANES), -1.0, jnp.float32) for _ in range(n // LANES)]
    for a in range(0, n, STEP):
        x1, x2 = c1[a : a + STEP, :], c2[a : a + STEP, :]
        for t in range(n // LANES):
            v = s[a : a + STEP, t * LANES : (t + 1) * LANES]
            y1, y2 = k1[:, t * LANES : (t + 1) * LANES], k2[:, t * LANES : (t + 1) * LANES]
            kept = jnp.where((x1 < y1) & (x2 < y2), v, -1.0)
            over[t] = jnp.maximum(over[t], jnp.max(kept.reshape(STEP // 8, 8, LANES), axis=0))
    best[...] = jnp.concatenate([jnp.max(o, axis=0, keepdims=True) for o in over], axis=1)


def lower_kernel(l1, l2, own, ownbest, keys, units, best, rowbest, c1, c2, s):
    n = own.shape[0]
    for p, src in enumerate((l1, l2)):
        normalise(src, units, p * n)
        c1[p * n : (p + 1) * n, :] = columns(keys[p : p + 1, :])
        c2[p * n : (p + 1) * n, :] = columns(keys[8 + p : 9 + p, :])
    rowbest[...] = jnp.full(rowbest.shape, -1.0, jnp.float32)
    score(units[...], own[...], s)
    best[...] = jnp.maximum(
        ownbest[...], pair_max(s, c1, c2, keys[2:3, :], keys[10:11, :], rowbest)
    )


def higher_kernel(h, units, rowbest, c1, c2, keys, hbest, l1best, l2best, unit, s, rb):
    n = h.shape[0]
    normalise(h, unit, 0)
    rb[...] = rowbest[...]
    score(units[...], unit[...], s)
    hbest[...] = pair_max(s, c1, c2, keys[4:5, :], keys[12:13, :], rb)
    l1best[...] = to_row(rb[:n, :])
    l2best[...] = to_row(rb[n:, :])


def call(kernel, outs, scratch, *args):
    return pl.pallas_call(
        kernel,
        out_shape=outs,
        in_specs=[VMEM] * len(args),
        out_specs=[VMEM] * len(outs),
        scratch_shapes=scratch,
        compiler_params=pltpu.CompilerParams(vmem_limit_bytes=16 << 20),
    )(*args)


def local(embeddings, sizes, order):
    n, width = embeddings.shape
    devices = lax.axis_size("row")
    me = lax.axis_index("row")
    l1 = shifted(embeddings, 2)
    h = shifted(embeddings, -2)
    l2 = shifted(embeddings, 1)

    f32 = functools.partial(jax.ShapeDtypeStruct, dtype=jnp.float32)
    b16 = functools.partial(jax.ShapeDtypeStruct, dtype=jnp.bfloat16)
    ends = jnp.cumsum(sizes)
    index = (me - 2) * n + jnp.arange(5 * n, dtype=jnp.int32)
    cluster = jnp.sum((index[:, None] >= ends[None, :]).astype(jnp.int32), axis=1)
    cluster = jnp.where(index < 0, -1, cluster).reshape(5, n)
    rank = jnp.stack(
        [
            lax.dynamic_slice_in_dim(order, jnp.clip(me + d, 0, devices - 1) * n, n, 0)
            for d in range(-2, 3)
        ]
    )
    items = devices * n
    k1 = jnp.pad(rank - items * cluster, ((0, 3), (0, 0)))
    k2 = jnp.pad(rank + items * cluster, ((0, 3), (0, 0)))
    keys = jnp.concatenate([k1, k2]).astype(jnp.float32)

    sq, tall = pltpu.VMEM((n, n), jnp.float32), pltpu.VMEM((2 * n, n), jnp.float32)
    col = pltpu.VMEM((n, LANES), jnp.float32)
    unit, best = call(
        own_kernel, [b16((n, width)), f32((1, n))], [sq, col, col], embeddings, keys
    )
    wide = f32((2 * n, LANES))
    units, best, rowbest, c1, c2 = call(
        lower_kernel, [b16((2 * n, width)), f32((1, n)), wide, wide, wide], [tall],
        l1, l2, unit, best, keys,
    )
    hbest, l1best, l2best = call(
        higher_kernel, [f32((1, n))] * 3,
        [pltpu.VMEM((n, width), jnp.bfloat16), tall, pltpu.VMEM((2 * n, LANES), jnp.float32)],
        h, units, rowbest, c1, c2, keys,
    )
    for value, by in ((hbest, 2), (l1best, -2), (l2best, -1)):
        came = shifted(value, by)
        there = (me - by >= 0) & (me - by < devices)
        best = jnp.maximum(best, jnp.where(there, came, -1.0))
    return best.reshape(n)


def solution(mesh):
    return jax.shard_map(
        local,
        mesh=mesh,
        in_specs=(P(("parts", "row"), None), P("parts"), P("parts")),
        out_specs=P(("parts", "row")),
        check_vma=False,
    )
```

time: 83.1 us -> 44.8 us (0.54)
  the two profiles are of different devices: /device:TPU:1252 before, /device:TPU:37 now
where the time goes in v1:
time: 44.8 us; the launch traced here: 44.5 us
  starting transfers between devices  24 us (54%)
  waiting for transfers between devices  12.3 us (27%)
  local copies, waits for them, and re-layouts  2.73 us (6%)
  Pallas kernels  2.72 us (6%)
  other arithmetic  2.47 us (6%)
    ppermute x6, starting transfers between devices, shifted(): lax.ppermute(x, 'row', [(i, i + by) for i in range(devices) if 0 <= i + b...  24 us
    ppermute x6, waiting for transfers between devices, shifted(): lax.ppermute(x, 'row', [(i, i + by) for i in range(devices) if 0 <= i + b...  12.3 us
    pallas_call x3, Pallas kernels, call(): pl.pallas_call(kernel, out_shape=outs, in_specs=[VMEM] * len(args), out_s...  2.72 us
    reduce_sum x1, other arithmetic, local(): jnp.sum((index[:, None] >= ends[None, :]).astype(jnp.int32), axis=1)  1.58 us
    unnamed x2, local copies, waits for them, and re-layouts  1.04 us
  transfers between devices with their start and end apart: 6, of which 2 were waited for; matrix products, arithmetic and copies ran while one was open for 8% of the time, Pallas kernels for 4%

profile of v1, /device:TPU:37, one launch (start us, length us, event | category | flops | bytes accessed | tf_op | source)
XLA Modules:
  0.0 44.5 jit_solution(8056913858795089242)
XLA Ops:
  0.0 4.6 %collective-permute-start = (bf16[512,512]{1,0:T(8,128)(2,1)}, bf16[512,512]{1,0:T(8,128)(2,1)S(1)}, u32[]{:S(2)}, u32[]{:S(2)}) collective-permute-start(bf16[512,512]{1,0:T(8,128)(2,1)} %own.1), channel_id=1, source_target_pairs={{0,2},{1,3},{2,4},{3,5},{4,6},{5,7},{6,8},{7,9},{8,10},{9,11},{10,... | collective-permute-start | bytes 1572872 | tf_op jit(solution)/shard_map/ppermute | solution.py:17
  4.6 4.5 %collective-permute-start.1 = (bf16[512,512]{1,0:T(8,128)(2,1)}, bf16[512,512]{1,0:T(8,128)(2,1)S(1)}, u32[]{:S(2)}, u32[]{:S(2)}) collective-permute-start(bf16[512,512]{1,0:T(8,128)(2,1)} %own.1), channel_id=1, source_target_pairs={{0,1},{1,2},{2,3},{3,4},{4,5},{5,6},{6,7},{7,8},{8,9},{9,10},{10,1... | collective-permute-start | bytes 1572872 | tf_op jit(solution)/shard_map/ppermute | solution.py:17
  9.2 1.3 %collective-permute-start.2 = (bf16[512,512]{1,0:T(8,128)(2,1)}, bf16[512,512]{1,0:T(8,128)(2,1)S(1)}, u32[]{:S(2)}, u32[]{:S(2)}) collective-permute-start(bf16[512,512]{1,0:T(8,128)(2,1)} %own.1), channel_id=1, source_target_pairs={{2,0},{3,1},{4,2},{5,3},{6,4},{7,5},{8,6},{9,7},{10,8},{11,9},{12,... | collective-permute-start | bytes 1572872 | tf_op jit(solution)/shard_map/ppermute | solution.py:17
  10.5 0.8 %copy.6 = s32[128,1]{1,0:T(8,128)S(1)} copy(s32[128,1]{0,1:T(1,128)} %bitcast.12) | data formatting | bytes 1024 | tf_op jit(solution)/shard_map/reshape.24
  11.3 0.2 reduce-window.8
  11.4 0.1 reduce
  11.5 1.6 %convert_reduce_fusion = s32[2560]{0:T(1024)S(1)} fusion(s32[128]{0:T(128)S(1)} %reduce, s32[2560]{0:T(1024)S(1)} %iota_add_fusion), kind=kLoop, calls=%fused_computation | loop fusion | flops 980480 | bytes 20992 | tf_op jit(solution)/shard_map/reduce_sum | solution.py:119
  13.1 0.9 %fusion.6 = (s32[512]{0:T(512)S(1)}, s32[512]{0:T(512)S(1)}, s32[512]{0:T(512)S(1)}, s32[512]{0:T(512)S(1)}, s32[512]{0:T(512)S(1)}) fusion(s32[32768]{0:T(1024)} %param.5, s32[]{:T(128)S(6)} %select_n.44, s32[]{:T(128)S(6)} %select_n.42, s32[]{:T(128)S(6)} %select_n.41, s32[]{:T(128)S(6)} %select_n.40, s32[]{:T(128)S(6)} %select_n.43), kind=kLoop, calls=%fused_computation.14 | loop fusion | bytes 20500 | tf_op jit(solution)/shard_map/dynamic_slice | solution.py:123
  14.1 0.0 copy-start
  14.1 1.0 %copy-done = bf16[512,512]{1,0:T(8,128)(2,1)S(1)} copy-done((bf16[512,512]{1,0:T(8,128)(2,1)S(1)}, bf16[512,512]{1,0:T(8,128)(2,1)}, u32[]{:S(2)}) %copy-start) | copy-done | bytes 524312
  15.2 0.6 %shard_map.37 = (bf16[512,512]{1,0:T(8,128)(2,1)S(1)}, f32[1,512]{1,0:T(1,128)S(1)}) custom-call(bf16[512,512]{1,0:T(8,128)(2,1)S(1)} %copy-done, f32[16,512]{1,0:T(8,128)S(1)} %fusion.keys), custom_call_target="tpu_custom_call" | custom-call | tf_op jit(solution)/shard_map/pallas_call | solution.py:97
  15.8 0.0 collective-permute-done.l1
  15.8 8.9 %collective-permute-done.1.l2 = bf16[512,512]{1,0:T(8,128)(2,1)S(1)} collective-permute-done((bf16[512,512]{1,0:T(8,128)(2,1)}, bf16[512,512]{1,0:T(8,128)(2,1)S(1)}, u32[]{:S(2)}, u32[]{:S(2)}) %collective-permute-start.1) | collective-permute-done | bytes 524320 | tf_op jit(solution)/shard_map/ppermute | solution.py:17
  24.7 1.0 %shard_map.38 = (bf16[1024,512]{1,0:T(8,128)(2,1)S(1)}, f32[1,512]{1,0:T(1,128)S(1)}, f32[1024,128]{1,0:T(8,128)S(1)}, f32[1024,128]{1,0:T(8,128)S(1)}, f32[1024,128]{1,0:T(8,128)S(1)}) custom-call(bf16[512,512]{1,0:T(8,128)(2,1)S(1)} %collective-permute-done.l1, bf16[512,512]{1,0:T(8,128)(2,1)S(1)} %collective-permute-done.1.l2, ...), custom_call_target="tpu_custom_call" | custom-call | tf_op jit(solution)/shard_map/pallas_call | solution.py:97
  25.6 0.0 collective-permute-done.2.h
  25.7 1.1 %shard_map.39 = (f32[1,512]{1,0:T(1,128)S(1)}, f32[1,512]{1,0:T(1,128)S(1)}, f32[1,512]{1,0:T(1,128)S(1)}) custom-call(bf16[512,512]{1,0:T(8,128)(2,1)S(1)} %collective-permute-done.2.h, bf16[1024,512]{1,0:T(8,128)(2,1)S(1)} %get-tuple-element.18.units, f32[1024,128]{1,0:T(8,128)S(1)} %get-tuple-element.19.rowbest, f32[1024,128]{1,0:T(8,128)S(1)} %get-tuple-element.20.c1, ...), custom_call_target="tpu_custom_call" | custom-call | tf_op jit(solution)/shard_map/pallas_call | solution.py:97
  26.8 2.2 %collective-permute-start.3 = (f32[1,512]{1,0:T(1,128)S(1)}, f32[1,512]{1,0:T(1,128)S(1)}, u32[]{:S(2)}, u32[]{:S(2)}) collective-permute-start(f32[1,512]{1,0:T(1,128)S(1)} %get-tuple-element.22), channel_id=1, source_target_pairs={{0,2},{1,3},{2,4},{3,5},{4,6},{5,7},{6,8},{7,9},{8,10},{9,11},{10,... | collective-permute-start | bytes 6152 | tf_op jit(solution)/shard_map/ppermute | solution.py:17
  29.0 1.3 %collective-permute-start.4 = (f32[1,512]{1,0:T(1,128)S(1)}, f32[1,512]{1,0:T(1,128)S(1)}, u32[]{:S(2)}, u32[]{:S(2)}) collective-permute-start(f32[1,512]{1,0:T(1,128)S(1)} %get-tuple-element.23), channel_id=1, source_target_pairs={{2,0},{3,1},{4,2},{5,3},{6,4},{7,5},{8,6},{9,7},{10,8},{11,9},{12,... | collective-permute-start | bytes 6152 | tf_op jit(solution)/shard_map/ppermute | solution.py:17
  30.3 10.1 %collective-permute-start.5 = (f32[1,512]{1,0:T(1,128)S(1)}, f32[1,512]{1,0:T(1,128)S(1)}, u32[]{:S(2)}, u32[]{:S(2)}) collective-permute-start(f32[1,512]{1,0:T(1,128)S(1)} %get-tuple-element.24), channel_id=1, source_target_pairs={{1,0},{2,1},{3,2},{4,3},{5,4},{6,5},{7,6},{8,7},{9,8},{10,9},{11,1... | collective-permute-start | bytes 6152 | tf_op jit(solution)/shard_map/ppermute | solution.py:17
  40.4 0.0 collective-permute-done.3
  40.4 0.0 collective-permute-done.4
  40.4 3.5 %collective-permute-done.5 = f32[1,512]{1,0:T(1,128)S(1)} collective-permute-done((f32[1,512]{1,0:T(1,128)S(1)}, f32[1,512]{1,0:T(1,128)S(1)}, u32[]{:S(2)}, u32[]{:S(2)}) %collective-permute-start.5) | collective-permute-done | bytes 2080 | tf_op jit(solution)/shard_map/ppermute | solution.py:17
  43.9 0.6 %fusion.5 = f32[1,512]{1,0:T(1,128)} fusion(f32[1,512]{1,0:T(1,128)S(1)} %get-tuple-element.17, f32[1,512]{1,0:T(1,128)S(1)} %collective-permute-done.3, pred[]{:T(512)S(6)} %and.10, f32[1,512]{1,0:T(1,128)S(1)} %collective-permute-done.4, pred[]{:T(512)S(6)} %and.11, f32[1,512]{1,0:T(1,128)S(1)} %collective-permute-done.5, pred[]{:T(512)S(6)} %and.12), kind=kLoop, calls=%fused_computation.13 | loop fusion | flops 3072 | bytes 10243 | tf_op jit(solution)/shard_map/max | solution.py:150
  (5 shorter events, 0.1 us)
Async XLA Ops:
  0.0 15.8 %collective-permute-start = (bf16[512,512]{1,0:T(8,128)(2,1)}, bf16[512,512]{1,0:T(8,128)(2,1)S(1)}, u32[]{:S(2)}, u32[]{:S(2)}) collective-permute-start(bf16[512,512]{1,0:T(8,128)(2,1)} %own.1), channel_id=1, source_target_pairs={{0,2},{1,3},{2,4},{3,5},{4,6},{5,7},{6,8},{7,9},{8,10},{9,11},{10,... | collective-permute-start | bytes 1572872 | tf_op jit(solution)/shard_map/ppermute | solution.py:17
  4.6 20.0 %collective-permute-start.1 = (bf16[512,512]{1,0:T(8,128)(2,1)}, bf16[512,512]{1,0:T(8,128)(2,1)S(1)}, u32[]{:S(2)}, u32[]{:S(2)}) collective-permute-start(bf16[512,512]{1,0:T(8,128)(2,1)} %own.1), channel_id=1, source_target_pairs={{0,1},{1,2},{2,3},{3,4},{4,5},{5,6},{6,7},{7,8},{8,9},{9,10},{10,1... | collective-permute-start | bytes 1572872 | tf_op jit(solution)/shard_map/ppermute | solution.py:17
  9.2 16.5 %collective-permute-start.2 = (bf16[512,512]{1,0:T(8,128)(2,1)}, bf16[512,512]{1,0:T(8,128)(2,1)S(1)}, u32[]{:S(2)}, u32[]{:S(2)}) collective-permute-start(bf16[512,512]{1,0:T(8,128)(2,1)} %own.1), channel_id=1, source_target_pairs={{2,0},{3,1},{4,2},{5,3},{6,4},{7,5},{8,6},{9,7},{10,8},{11,9},{12,... | collective-permute-start | bytes 1572872 | tf_op jit(solution)/shard_map/ppermute | solution.py:17
  14.1 1.0 %copy-start = (bf16[512,512]{1,0:T(8,128)(2,1)S(1)}, bf16[512,512]{1,0:T(8,128)(2,1)}, u32[]{:S(2)}) copy-start(bf16[512,512]{1,0:T(8,128)(2,1)} %own.1) | copy-start | bytes 1572868
  26.8 13.6 %collective-permute-start.3 = (f32[1,512]{1,0:T(1,128)S(1)}, f32[1,512]{1,0:T(1,128)S(1)}, u32[]{:S(2)}, u32[]{:S(2)}) collective-permute-start(f32[1,512]{1,0:T(1,128)S(1)} %get-tuple-element.22), channel_id=1, source_target_pairs={{0,2},{1,3},{2,4},{3,5},{4,6},{5,7},{6,8},{7,9},{8,10},{9,11},{10,... | collective-permute-start | bytes 6152 | tf_op jit(solution)/shard_map/ppermute | solution.py:17
  29.0 11.4 %collective-permute-start.4 = (f32[1,512]{1,0:T(1,128)S(1)}, f32[1,512]{1,0:T(1,128)S(1)}, u32[]{:S(2)}, u32[]{:S(2)}) collective-permute-start(f32[1,512]{1,0:T(1,128)S(1)} %get-tuple-element.23), channel_id=1, source_target_pairs={{2,0},{3,1},{4,2},{5,3},{6,4},{7,5},{8,6},{9,7},{10,8},{11,9},{12,... | collective-permute-start | bytes 6152 | tf_op jit(solution)/shard_map/ppermute | solution.py:17
  30.3 13.6 %collective-permute-start.5 = (f32[1,512]{1,0:T(1,128)S(1)}, f32[1,512]{1,0:T(1,128)S(1)}, u32[]{:S(2)}, u32[]{:S(2)}) collective-permute-start(f32[1,512]{1,0:T(1,128)S(1)} %get-tuple-element.24), channel_id=1, source_target_pairs={{1,0},{2,1},{3,2},{4,3},{5,4},{6,5},{7,6},{8,7},{9,8},{10,9},{11,1... | collective-permute-start | bytes 6152 | tf_op jit(solution)/shard_map/ppermute | solution.py:17
